TPU v7x, 32 devices: a whole 2x2x4 slice. The times are simulated.
32 devices in a mesh: section: 4 (over z), expert: 4 (over y, x), dp: 2 (over core).
Axes of the slice: x: 2, y: 2, z: 4, core: 2. Of those that a mesh axis runs over, the one named last changes fastest.
Arguments:
- stash: bfloat16 [4, 256, 2048], P('section', 'dp', 'expert'), may hold values from -6 to 6
- cotangent: bfloat16 [4, 256, 2048], P('section', 'dp', 'expert'), may hold values from -6 to 6
- backward_expert_routes: int32 [4, 256, 2], P('section', 'dp'), may hold values from 0 to 3, all different within a row; in each aligned block of 128 rows (0 to 127, 128 to 255, ..., all dimensions but the last counted through in order) at most 80 rows name the same one
- backward_job_lengths: int32 [4, 4], P('section'), may hold values from 1 to 128, 256 in all within a row
- layer_norm_gains: float32 [4, 2048], P('section'), may hold values from 0.25 to 1.75
- router: bfloat16 [4, 2048, 4], P('section'), may hold values from -0.125 to 0.125
- expert_gate_weight: bfloat16 [4, 2048, 28672], P('section', None, ('expert', 'dp')), may hold values from -0.125 to 0.125
- expert_up_weight: bfloat16 [4, 2048, 28672], P('section', None, ('expert', 'dp')), may hold values from -0.125 to 0.125
- expert_down_weight: bfloat16 [4, 28672, 2048], P('section', ('expert', 'dp')), may hold values from -0.0625 to 0.0625
- adapter_down_maps: bfloat16 [4, 2048, 64], P('section', 'expert'), may hold values from -0.125 to 0.125
- adapter_up_maps: bfloat16 [4, 64, 2048], P('section', None, 'expert'), may hold values from -1.5 to 1.5
Outputs:
- handed_back: bfloat16 [4, 256, 2048], P('section', 'dp', 'expert')
- grad_lora_down: float32 [4, 2048, 64], P('section', 'expert')
- grad_lora_up: float32 [4, 64, 2048], P('section', None, 'expert')
Inputs may be any that keep to these rules, and one draw needn't show every extreme that they name: `backward_expert_routes`: each row names two different experts. In each aligned block of 128 rows (the tokens of one device) no expert is named more than 80 times. `backward_job_lengths`: each row sums to 256.
All inputs are finite; a program needn't handle non-finite values.
Results may differ from a plain program's by a relative error of at most 0.008.
Values may be sent and summed in bfloat16 or wider, within the bound.
A program may use at most 128 MiB of HBM per device.

v0:
```python
import jax
import jax.numpy as jnp
from jax import lax
from jax.sharding import PartitionSpec as P

MODEL_WIDTH = 2048
EXPERTS = 4
ADAPTER_RANK = 16
CAP = 80
EPS = 1e-05
ADAPTER_SCALE = 0.5
HIGH = lax.Precision.HIGHEST


def from_behind(block, axis, distance):
    devices = range(lax.axis_size(axis))
    route = [((i - distance) % len(devices), i) for i in devices]
    return lax.ppermute(block, axis, route)


def job_columns(job_token_lengths, offset, count):
    ends = jnp.cumsum(job_token_lengths, dtype=jnp.int32)
    position = offset + jnp.arange(count, dtype=jnp.int32)
    owner = jnp.sum((ends[None, :] <= position[:, None]).astype(jnp.int32), axis=1, dtype=jnp.int32)
    column_owner = (
        jnp.arange(job_token_lengths.shape[0] * ADAPTER_RANK, dtype=jnp.int32) // ADAPTER_RANK
    )
    return (owner[:, None] == column_owner[None, :]).astype(jnp.float32)


def prepare(whole_batch, norm_gain_vector, router, token_routes):
    expert_values = whole_batch.astype(jnp.float32)
    scale = lax.rsqrt(jnp.mean(expert_values * expert_values, axis=1, keepdims=True) + EPS)
    normalized_input = (expert_values * scale * norm_gain_vector[None, :]).astype(jnp.bfloat16)
    logits = jnp.dot(normalized_input, router, preferred_element_type=jnp.float32)
    labels = jnp.arange(router.shape[1], dtype=jnp.int32)
    first = (token_routes[:, 0:1] == labels[None, :]).astype(jnp.float32)
    second = (token_routes[:, 1:2] == labels[None, :]).astype(jnp.float32)
    upper = jax.nn.sigmoid(jnp.sum(first * logits, axis=1) - jnp.sum(second * logits, axis=1))
    table = upper[:, None] * first + (1.0 - upper)[:, None] * second
    return (expert_values, scale, normalized_input, first, second, upper, table)


def router_grad(gate_grad, first, second, upper):
    spread = jnp.sum(first * gate_grad, axis=1) - jnp.sum(second * gate_grad, axis=1)
    delta = spread * upper * (1.0 - upper)
    return delta[:, None] * (first - second)


def slot_matrix(member, capacity):
    marks = member.astype(jnp.int32)
    ranked = jnp.cumsum(marks, axis=-1, dtype=jnp.int32) - marks
    slots = jnp.arange(capacity, dtype=jnp.int32)
    hit = (ranked[..., None, :] == slots[:, None]) & (marks[..., None, :] == 1)
    return hit.astype(jnp.float32)


def expert_back(
    rows, adapter_gradient_list, expert_gate_weight, expert_up_weight, expert_down_weight
):
    gate = jnp.dot(rows, expert_gate_weight, preferred_element_type=jnp.float32)
    up = jnp.dot(rows, expert_up_weight, preferred_element_type=jnp.float32)
    sig = jax.nn.sigmoid(gate)
    act = gate * sig
    hidden = (act * up).astype(jnp.bfloat16)
    output = jnp.dot(hidden, expert_down_weight, preferred_element_type=jnp.float32)
    gate_term = jnp.sum(adapter_gradient_list.astype(jnp.float32) * output, axis=1)
    back = jnp.dot(adapter_gradient_list, expert_down_weight.T, preferred_element_type=jnp.float32)
    d_gate = (back * up * sig * (1.0 + gate * (1.0 - sig))).astype(jnp.bfloat16)
    d_up = (back * act).astype(jnp.bfloat16)
    d_rows = jnp.dot(d_gate, expert_gate_weight.T, preferred_element_type=jnp.float32) + jnp.dot(
        d_up, expert_up_weight.T, preferred_element_type=jnp.float32
    )
    return (d_rows, gate_term)


def body(
    stash,
    cotangent,
    backward_expert_routes,
    backward_job_lengths,
    layer_norm_gains,
    router,
    expert_gate_weight,
    expert_up_weight,
    expert_down_weight,
    adapter_down_maps,
    adapter_up_maps,
):
    groups = lax.axis_size("expert")
    shards = lax.axis_size("dp")
    column_block = lax.axis_index("expert")
    token_block = lax.axis_index("dp")
    mine = column_block // (groups // EXPERTS)
    s_cols = stash[0]
    gradient_columns = cotangent[0]
    count, width = s_cols.shape
    s_full, g_full = (
        lax.all_gather(s_cols, "expert", axis=1, tiled=True),
        lax.all_gather(gradient_columns, "expert", axis=1, tiled=True),
    )
    norm_gain_vector = layer_norm_gains[0]
    route_w = router[0]
    wg = expert_gate_weight[0]
    wu = expert_up_weight[0]
    wd = expert_down_weight[0]
    down_map_rows = adapter_down_maps[0]
    backward_columns = adapter_up_maps[0]
    col_start = column_block * width
    gain_cols = lax.dynamic_slice_in_dim(norm_gain_vector, col_start, width, 0)
    route_cols = lax.dynamic_slice_in_dim(route_w, col_start, width, 0)
    offset = token_block * count
    backward_mask = job_columns(backward_job_lengths[0], offset, count)
    b_values, b_scale, b_normed, b_first, b_second, b_upper, b_table = prepare(
        s_full, norm_gain_vector, route_w, backward_expert_routes[0]
    )
    labels = jnp.arange(EXPERTS, dtype=jnp.int32)
    own = (labels == mine).astype(jnp.float32)
    b_member = jnp.sum((b_first + b_second) * own[None, :], axis=1)
    b_gate = jnp.sum(b_table * own[None, :], axis=1)
    b_slots = slot_matrix(b_member, CAP)
    b_normed_cols = lax.dynamic_slice_in_dim(b_normed, col_start, width, 1)
    a_full = lax.all_gather(down_map_rows, "expert", axis=0, tiled=True)
    b_low = jnp.dot(b_normed, a_full, preferred_element_type=jnp.float32)
    grad_low_rank = lax.psum(
        jnp.dot(gradient_columns, backward_columns.T, preferred_element_type=jnp.float32), "expert"
    )
    backward_low_rank = (b_low * backward_mask).astype(jnp.bfloat16)
    grad_low_rank_backward = (ADAPTER_SCALE * grad_low_rank * backward_mask).astype(jnp.bfloat16)
    up_map_gradient = ADAPTER_SCALE * jnp.dot(
        backward_low_rank.T, gradient_columns, preferred_element_type=jnp.float32
    )
    down_map_gradient = jnp.dot(
        b_normed_cols.T, grad_low_rank_backward, preferred_element_type=jnp.float32
    )
    down_map_gradient, up_map_gradient = lax.psum((down_map_gradient, up_map_gradient), "dp")
    normalized_grad_adapter = jnp.dot(
        grad_low_rank_backward, down_map_rows.T, preferred_element_type=jnp.float32
    )
    b_slots_low = b_slots.astype(jnp.bfloat16)
    b_sel = jnp.dot(b_slots_low, b_normed, preferred_element_type=jnp.float32).astype(jnp.bfloat16)
    g_sel = jnp.dot(b_slots_low, g_full, preferred_element_type=jnp.float32).astype(jnp.bfloat16)
    b_rows, g_rows = (
        lax.all_gather(b_sel, "dp", axis=0, tiled=True),
        lax.all_gather(g_sel, "dp", axis=0, tiled=True),
    )
    dn_slots, dgam_slots = expert_back(b_rows, g_rows, wg, wu, wd)
    b_member_all, b_gate_all = (
        lax.all_gather(b_member, "dp", axis=0, tiled=True),
        lax.all_gather(b_gate, "dp", axis=0, tiled=True),
    )
    b_all = slot_matrix(b_member_all.reshape(shards, count), CAP)
    b_terms = jnp.einsum(
        "pct,pcex->eptx", b_all, dn_slots.reshape(shards, CAP, groups, width), precision=HIGH
    )
    b_terms = b_terms * b_gate_all.reshape(shards, count)[None, :, :, None]
    normalized_grad_experts = lax.psum_scatter(
        b_terms.reshape(groups * shards * count, width),
        ("expert", "dp"),
        scatter_dimension=0,
        tiled=True,
    )
    dgam_own = lax.psum_scatter(dgam_slots, "dp", scatter_dimension=0, tiled=True)
    dgam_tokens = jnp.dot(dgam_own, b_slots, precision=HIGH)
    gate_part = dgam_tokens[:, None] * own[None, :]
    expert_base_output = normalized_grad_experts + normalized_grad_adapter
    b_values_cols = lax.dynamic_slice_in_dim(b_values, col_start, width, 1)
    route_cols_t = route_cols.astype(jnp.float32).T
    base_weighted = expert_base_output * gain_cols[None, :]
    stat_part = jnp.sum(base_weighted * b_values_cols, axis=1, keepdims=True)
    gate_grad, stat_part = lax.psum((gate_part, stat_part), "expert")
    d_logit = router_grad(gate_grad, b_first, b_second, b_upper)
    lifted = jnp.dot(
        b_values * norm_gain_vector[None, :], route_w.astype(jnp.float32), precision=HIGH
    )
    stat = stat_part + jnp.sum(d_logit * lifted, axis=1, keepdims=True)
    weighted = base_weighted + jnp.dot(d_logit, route_cols_t, precision=HIGH) * gain_cols[None, :]
    layer_result = (
        gradient_columns.astype(jnp.float32)
        + b_scale * weighted
        - b_values_cols * b_scale * b_scale * b_scale * stat / MODEL_WIDTH
    )
    handed_back = from_behind(layer_result.astype(jnp.bfloat16), "section", -1)
    return (handed_back[None], down_map_gradient[None], up_map_gradient[None])


def solution(mesh):
    return jax.shard_map(
        body,
        mesh=mesh,
        in_specs=(
            P("section", "dp", "expert"),
            P("section", "dp", "expert"),
            P("section", "dp", None),
            P("section", None),
            P("section", None),
            P("section", None, None),
            P("section", None, ("expert", "dp")),
            P("section", None, ("expert", "dp")),
            P("section", ("expert", "dp"), None),
            P("section", "expert", None),
            P("section", None, "expert"),
        ),
        out_specs=(
            P("section", "dp", "expert"),
            P("section", "expert", None),
            P("section", None, "expert"),
        ),
        check_vma=False,
    )
```

profile of v0, /device:TPU:0, one launch (start us, length us, event | category | flops | bytes accessed | tf_op | source)
XLA Modules:
  0.0 168.8 jit_solution(5793704472606777799)
XLA Ops:
  8.1 12.0 %all-gather = bf16[1,128,2048]{2,1,0:T(8,128)(2,1)S(1)} all-gather(bf16[1,128,512]{2,1,0:T(8,128)(2,1)} %param.11), channel_id=2, replica_groups=mesh['section'=4,'expert'=4,'dp'=2] {'expert'}, dimensions={2}, use_global_device_ids=true | all-gather | bytes 655360 | tf_op jit(solution)/shard_map/all_gather | solution.py:99
  20.3 0.8 slice_bitcast_fusion.1
  21.0 0.9 fusion.35
  21.9 1.0 select_reduce_fusion.2
  23.0 1.8 %all-gather.3 = f32[2,1,128]{2,1,0:T(1,128)S(1)} all-gather(f32[1,1,128]{2,1,0:T(1,128)S(1)} %bitcast.144), channel_id=1, replica_groups=mesh['section'=4,'expert'=4,'dp'=2] {'dp'}, dimensions={0}, use_global_device_ids=true | all-gather | bytes 1536 | tf_op jit(solution)/shard_map/all_gather | solution.py:149
  25.3 9.7 %all-gather.1 = bf16[1,128,2048]{2,1,0:T(8,128)(2,1)S(1)} all-gather(bf16[1,128,512]{2,1,0:T(8,128)(2,1)S(1)} %copy-done.2), channel_id=3, replica_groups=mesh['section'=4,'expert'=4,'dp'=2] {'expert'}, dimensions={2}, use_global_device_ids=true | all-gather | bytes 655360 | tf_op jit(solution)/shard_map/all_gather | solution.py:100
  35.4 2.3 %all_gather.23 = bf16[160,2048]{1,0:T(8,128)(2,1)S(1)} all-gather(bf16[80,2048]{1,0:T(8,128)(2,1)S(1)} %convolution_convert_fusion.1), channel_id=1, replica_groups=mesh['section'=4,'expert'=4,'dp'=2] {'dp'}, dimensions={0}, use_global_device_ids=true | all-gather | bytes 983040 | tf_op jit(solution)/shard_map/all_gather | solution.py:145
  37.7 2.3 %all_gather.24 = bf16[160,2048]{1,0:T(8,128)(2,1)S(1)} all-gather(bf16[80,2048]{1,0:T(8,128)(2,1)S(1)} %convolution_convert_fusion), channel_id=1, replica_groups=mesh['section'=4,'expert'=4,'dp'=2] {'dp'}, dimensions={0}, use_global_device_ids=true | all-gather | bytes 983040 | tf_op jit(solution)/shard_map/all_gather | solution.py:144
  40.0 9.3 %fusion.2 = f32[160,3584]{1,0:T(8,128)} fusion(bf16[160,2048]{1,0:T(8,128)(2,1)S(1)} %all_gather.24, bf16[1,2048,3584]{2,1,0:T(8,128)(2,1)} %param.17), kind=kOutput, calls=%fused_computation.2 | convolution fusion | flops 2348810240 | bytes 17629184 | tf_op jit(solution)/shard_map/dot_general | solution.py:61
  49.3 0.9 copy-done.1
  50.1 3.9 %fusion.6 = f32[160,3584]{1,0:T(8,128)} fusion(bf16[160,2048]{1,0:T(8,128)(2,1)S(1)} %all_gather.24, bf16[1,2048,3584]{2,1,0:T(8,128)(2,1)S(1)} %copy-done.1), kind=kOutput, calls=%fused_computation.6 | convolution fusion | flops 2348810240 | bytes 17629184 | tf_op jit(solution)/shard_map/dot_general | solution.py:62
  54.1 11.6 %fusion.10 = f32[160,3584]{1,0:T(8,128)} fusion(bf16[160,2048]{1,0:T(8,128)(2,1)S(1)} %all_gather.23, bf16[1,3584,2048]{2,1,0:T(8,128)(2,1)} %param.19), kind=kOutput, calls=%fused_computation.10 | convolution fusion | flops 2348810240 | bytes 17629184 | tf_op jit(solution)/shard_map/dot_general | solution.py:68
  65.7 12.1 %fusion = f32[160,2048]{1,0:T(8,128)S(1)} fusion(bf16[1,2048,3584]{2,1,0:T(8,128)(2,1)} %param.17, f32[160,3584]{1,0:T(8,128)} %fusion.2, f32[160,3584]{1,0:T(8,128)} %fusion.10, f32[160,3584]{1,0:T(8,128)} %fusion.6), kind=kOutput, calls=%fused_computation | convolution fusion | flops 2354544640 | bytes 22872064 | tf_op jit(solution)/shard_map/dot_general | solution.py:71
  77.8 12.7 %fusion.15 = f32[160,2048]{1,0:T(8,128)} fusion(f32[160,2048]{1,0:T(8,128)S(1)} %fusion, bf16[1,2048,3584]{2,1,0:T(8,128)(2,1)} %param.18, f32[160,3584]{1,0:T(8,128)} %fusion.10, f32[160,3584]{1,0:T(8,128)} %fusion.2), kind=kOutput, calls=%fused_computation.13 | convolution fusion | flops 2352578560 | bytes 21889024 | tf_op jit(solution)/shard_map/dot_general | solution.py:71
  90.5 2.2 %reshape.159 = f32[2,80,4,512]{3,2,1,0:T(4,128)S(1)} reshape(f32[160,2048]{1,0:T(8,128)} %fusion.15) | data formatting | bytes 2621440 | tf_op jit(solution)/shard_map/reshape | solution.py:154
  93.0 1.8 %all-gather.4 = f32[2,1,128]{2,1,0:T(1,128)S(1)} all-gather(f32[1,1,128]{2,1,0:T(1,128)S(1)} %bitcast.143), channel_id=1, replica_groups=mesh['section'=4,'expert'=4,'dp'=2] {'dp'}, dimensions={0}, use_global_device_ids=true | all-gather | bytes 1536 | tf_op jit(solution)/shard_map/all_gather | solution.py:150
  94.8 1.5 multiply_bitcast_fusion
  96.4 1.6 copy.28
  98.4 15.4 %psum.35 = f32[128,64]{0,1:T(8,128)S(1)} all-reduce(f32[128,64]{0,1:T(8,128)S(1)} %fusion.48), channel_id=1, replica_groups=mesh['section'=4,'expert'=4,'dp'=2] {'expert'}, use_global_device_ids=true, to_apply=%region_10.11 | all-reduce | flops 8192 | bytes 65536 | tf_op jit(solution)/shard_map/psum | solution.py:125
  113.8 9.4 %all-gather.2 = bf16[1,2048,64]{1,2,0:T(8,128)(2,1)S(1)} all-gather(bf16[1,512,64]{1,2,0:T(8,128)(2,1)S(1)} %copy-done.3), channel_id=4, replica_groups=mesh['section'=4,'expert'=4,'dp'=2] {'expert'}, dimensions={1}, use_global_device_ids=true | all-gather | bytes 327680 | tf_op jit(solution)/shard_map/all_gather | solution.py:123
  123.3 0.9 convolution_bitcast_fusion
  124.2 1.1 fusion.30
  125.3 9.5 %fusion.20 = f32[160]{0:T(256)S(1)} fusion(bf16[1,3584,2048]{2,1,0:T(8,128)(2,1)} %param.19, bf16[160,2048]{1,0:T(8,128)(2,1)S(1)} %all_gather.23, f32[160,3584]{1,0:T(8,128)} %fusion.6, f32[160,3584]{1,0:T(8,128)} %fusion.2), kind=kOutput, calls=%fused_computation.23 | convolution fusion | flops 2353233664 | bytes 19923584 | tf_op jit(solution)/shard_map/dot_general | solution.py:66
  135.0 2.5 %all-reduce = f32[160]{0:T(256)S(1)} all-reduce(f32[160]{0:T(256)S(1)} %fusion.20), channel_id=6, replica_groups=mesh['section'=4,'expert'=4,'dp'=2] {'dp'}, use_global_device_ids=true, to_apply=%region_12.13.clone | all-reduce | flops 160 | bytes 1280
  139.0 1.3 reduce-scatter.2.cloned.1.call-done
  140.3 1.3 fusion.47
  141.6 8.9 %all-reduce.1 = (f32[128,1]{0,1:T(1,128)S(1)}, f32[128,4]{0,1:T(4,128)S(1)}) all-reduce(f32[128,1]{0,1:T(1,128)S(1)} %bitcast.140, f32[128,4]{0,1:T(4,128)S(1)} %broadcast_multiply_fusion), channel_id=1, replica_groups=mesh['section'=4,'expert'=4,'dp'=2] {'expert'}, use_global_device_ids=true, to_apply=%region_17.18 | all-reduce | flops 640 | bytes 5120 | tf_op jit(solution)/shard_map/psum | solution.py:171
  150.6 0.7 fusion.32
  151.6 3.4 %collective-permute-start = (bf16[128,512]{1,0:T(8,128)(2,1)S(1)}, bf16[128,512]{1,0:T(8,128)(2,1)S(1)}, u32[]{:S(2)}, u32[]{:S(2)}) collective-permute-start(bf16[128,512]{1,0:T(8,128)(2,1)S(1)} %fusion.28), channel_id=1, source_target_pairs={{8,0},{16,8},{24,16},{0,24},{9,1},{17,9},{25,17},{1,25},{10,2},{18... | collective-permute-start | bytes 393224 | tf_op jit(solution)/shard_map/ppermute | solution.py:18
  155.1 2.5 %collective-permute-done = bf16[128,512]{1,0:T(8,128)(2,1)S(1)} collective-permute-done((bf16[128,512]{1,0:T(8,128)(2,1)S(1)}, bf16[128,512]{1,0:T(8,128)(2,1)S(1)}, u32[]{:S(2)}, u32[]{:S(2)}) %collective-permute-start) | collective-permute-done | bytes 131104 | tf_op jit(solution)/shard_map/ppermute | solution.py:18
  158.2 1.6 copy.36
  159.8 1.6 copy.37
  (52 shorter events, 4.1 us)
Async XLA Ops:
  8.0 90.3 %copy-start = (bf16[1,64,512]{2,1,0:T(8,128)(2,1)S(1)}, bf16[1,64,512]{2,1,0:T(8,128)(2,1)}, u32[]{:S(2)}) copy-start(bf16[1,64,512]{2,1,0:T(8,128)(2,1)} %param.21) | copy-start | bytes 196612
  8.0 17.2 %copy-start.2 = (bf16[1,128,512]{2,1,0:T(8,128)(2,1)S(1)}, bf16[1,128,512]{2,1,0:T(8,128)(2,1)}, u32[]{:S(2)}) copy-start(bf16[1,128,512]{2,1,0:T(8,128)(2,1)} %param.12) | copy-start | bytes 393220
  8.0 132.3 %reduce-scatter.2.cloned.1.call-start = ((), (), s32[]{:S(2)}) async-start(), calls=%async_computation.1 | async-start | bytes 2359296 | tf_op jit(solution)/shard_map/reduce_scatter | solution.py:157
  40.0 10.2 %copy-start.1 = (bf16[1,2048,3584]{2,1,0:T(8,128)(2,1)S(1)}, bf16[1,2048,3584]{2,1,0:T(8,128)(2,1)}, u32[]{:S(2)}) copy-start(bf16[1,2048,3584]{2,1,0:T(8,128)(2,1)} %param.18) | copy-start | bytes 44040196
  96.4 1.7 %copy-start.6 = (s32[1,4]{1,0:T(1,128)S(1)}, s32[1,4]{1,0:T(1,128)}, u32[]{:S(2)}) copy-start(s32[1,4]{1,0:T(1,128)} %param.14) | copy-start | bytes 52
  96.4 17.4 %copy-start.3 = (bf16[1,512,64]{1,2,0:T(8,128)(2,1)S(1)}, bf16[1,512,64]{1,2,0:T(8,128)(2,1)}, u32[]{:S(2)}) copy-start(bf16[1,512,64]{1,2,0:T(8,128)(2,1)} %param.20) | copy-start | bytes 196612
  98.0 59.6 %all-reduce.5.cloned.1.call-start = ((), (), s32[]{:S(2)}) async-start(), calls=%async_computation.2 | async-start | bytes 524288 | tf_op jit(solution)/shard_map/psum | solution.py:136
  125.3 9.6 %copy-start.5 = (f32[1,2048]{1,0:T(1,128)S(1)}, f32[1,2048]{1,0:T(1,128)}, u32[]{:S(2)}) copy-start(f32[1,2048]{1,0:T(1,128)} %param.15) | copy-start | bytes 24580
  125.3 12.2 %copy-start.7 = (u32[32]{0:T(128)S(1)}, u32[32]{0:T(128)}, u32[]{:S(2)}) copy-start(u32[32]{0:T(128)} %constant.94) | copy-start | bytes 388
  134.9 15.7 %copy-start.4 = (bf16[1,2048,4]{1,2,0:T(4,128)(2,1)S(1)}, bf16[1,2048,4]{1,2,0:T(4,128)(2,1)}, u32[]{:S(2)}) copy-start(bf16[1,2048,4]{1,2,0:T(4,128)(2,1)} %param.16) | copy-start | bytes 49156
  151.6 6.0 %collective-permute-start = (bf16[128,512]{1,0:T(8,128)(2,1)S(1)}, bf16[128,512]{1,0:T(8,128)(2,1)S(1)}, u32[]{:S(2)}, u32[]{:S(2)}) collective-permute-start(bf16[128,512]{1,0:T(8,128)(2,1)S(1)} %fusion.28), channel_id=1, source_target_pairs={{8,0},{16,8},{24,16},{0,24},{9,1},{17,9},{25,17},{1,25},{10,2},{18... | collective-permute-start | bytes 393224 | tf_op jit(solution)/shard_map/ppermute | solution.py:18
Sparse Core Ops, SparseCore 0:
  98.1 42.1 reduce-scatter.1
Sparse Core Ops, SparseCore 1:
  125.4 18.3 all-reduce.4
where the time goes:
time: 169 us
  matrix products  66.8 us (40%)
  blocking collectives  66 us (39%)
  between operations  16.4 us (10%)
  local copies, waits for them, and re-layouts  9.96 us (6%)
  waiting for transfers between devices  3.87 us (2%)
  starting transfers between devices  3.51 us (2%)
  other arithmetic  2.28 us (1%)
    psum x1, blocking collectives, body(): lax.psum(jnp.dot(gradient_columns, backward_columns.T, preferred_element_...  15.4 us
    dot_general x1, matrix products, expert_back(): jnp.dot(d_up, expert_up_weight.T, preferred_element_type=jnp.float32)  12.7 us
    dot_general x1, matrix products, expert_back(): jnp.dot(d_gate, expert_gate_weight.T, preferred_element_type=jnp.float32)  12.1 us
    all_gather x1, blocking collectives, body(): lax.all_gather(s_cols, 'expert', axis=1, tiled=True)  12 us
    dot_general x1, matrix products, expert_back(): jnp.dot(adapter_gradient_list, expert_down_weight.T, preferred_element_ty...  11.6 us
    all_gather x1, blocking collectives, body(): lax.all_gather(gradient_columns, 'expert', axis=1, tiled=True)  9.67 us
    dot_general x1, matrix products, expert_back(): jnp.dot(hidden, expert_down_weight, preferred_element_type=jnp.float32)  9.53 us
    all_gather x1, blocking collectives, body(): a_full = lax.all_gather(down_map_rows, 'expert', axis=0, tiled=True)  9.38 us
  transfers between devices with their start and end apart: 3, of which 2 were waited for; matrix products, arithmetic and copies ran while one was open for 9% of the time, Pallas kernels for 0%

commit v1 on v0

--- a/solution.py
+++ b/solution.py
@@ -10,6 +10,10 @@
 EPS = 1e-05
 ADAPTER_SCALE = 0.5
 HIGH = lax.Precision.HIGHEST
+
+
+def sections_play(inner_x, group_axis):
+    return jnp.concatenate(jax.lax.all_gather(inner_x, axis_name=group_axis), axis=1)
 
 
 def from_behind(block, axis, distance):
@@ -96,7 +100,7 @@
     gradient_columns = cotangent[0]
     count, width = s_cols.shape
     s_full, g_full = (
-        lax.all_gather(s_cols, "expert", axis=1, tiled=True),
+        sections_play(s_cols, "expert"),
         lax.all_gather(gradient_columns, "expert", axis=1, tiled=True),
     )
     norm_gain_vector = layer_norm_gains[0]

time: 169 us -> 173 us (1.024)
  other arithmetic: 2.28 us -> 4.87 us
    unnamed x20 -> x49, local copies, waits for them, and re-layouts: 5.31 us -> 4.97 us
where the time goes in v1:
time: 173 us; the launch traced here: 172 us
  blocking collectives  67.1 us (39%)
  matrix products  66 us (38%)
  between operations  16.5 us (10%)
  local copies, waits for them, and re-layouts  10.4 us (6%)
  other arithmetic  4.87 us (3%)
  waiting for transfers between devices  3.95 us (2%)
  starting transfers between devices  3.48 us (2%)
    psum x1, blocking collectives, body(): lax.psum(jnp.dot(gradient_columns, backward_columns.T, preferred_element_...  15.4 us
    dot_general x1, matrix products, expert_back(): jnp.dot(d_up, expert_up_weight.T, preferred_element_type=jnp.float32)  12.8 us
    dot_general x1, matrix products, expert_back(): jnp.dot(d_gate, expert_gate_weight.T, preferred_element_type=jnp.float32)  12.1 us
    all_gather x1, blocking collectives, sections_play(): jax.lax.all_gather(inner_x, axis_name=group_axis)  11.9 us
    dot_general x1, matrix products, expert_back(): jnp.dot(adapter_gradient_list, expert_down_weight.T, preferred_element_ty...  11.6 us
    all_gather x1, blocking collectives, body(): lax.all_gather(gradient_columns, 'expert', axis=1, tiled=True)  10.3 us
    dot_general x1, matrix products, expert_back(): jnp.dot(hidden, expert_down_weight, preferred_element_type=jnp.float32)  9.67 us
    all_gather x1, blocking collectives, body(): a_full = lax.all_gather(down_map_rows, 'expert', axis=0, tiled=True)  9.37 us
  transfers between devices with their start and end apart: 3, of which 2 were waited for; matrix products, arithmetic and copies ran while one was open for 9% of the time, Pallas kernels for 0%

profile of v1, /device:TPU:0, one launch (start us, length us, event | category | flops | bytes accessed | tf_op | source)
XLA Modules:
  0.0 172.3 jit_solution(14432971408479305235)
XLA Ops:
  8.1 11.9 %all_gather.21 = bf16[4,128,512]{2,1,0:T(8,128)(2,1)S(1)} all-gather(bf16[1,128,512]{2,1,0:T(8,128)(2,1)} %param.11), channel_id=1, replica_groups=mesh['section'=4,'expert'=4,'dp'=2] {'expert'}, dimensions={0}, use_global_device_ids=true | all-gather | bytes 655360 | tf_op jit(solution)/shard_map/all_gather | solution.py:16
  21.2 0.7 reduce.6
  21.9 1.4 convert_multiply_fusion
  23.6 1.9 %all-gather.2 = f32[2,1,128]{2,1,0:T(1,128)S(1)} all-gather(f32[1,1,128]{2,1,0:T(1,128)S(1)} %bitcast.131), channel_id=1, replica_groups=mesh['section'=4,'expert'=4,'dp'=2] {'dp'}, dimensions={0}, use_global_device_ids=true | all-gather | bytes 1536 | tf_op jit(solution)/shard_map/all_gather | solution.py:153
  25.5 10.3 %all-gather = bf16[1,128,2048]{2,1,0:T(8,128)(2,1)} all-gather(bf16[1,128,512]{2,1,0:T(8,128)(2,1)S(1)} %copy-done.4), channel_id=2, replica_groups=mesh['section'=4,'expert'=4,'dp'=2] {'expert'}, dimensions={2}, use_global_device_ids=true | all-gather | bytes 655360 | tf_op jit(solution)/shard_map/all_gather | solution.py:104
  35.8 1.3 copy.37
  37.2 1.9 %all-gather.3 = f32[2,1,128]{2,1,0:T(1,128)S(1)} all-gather(f32[1,1,128]{2,1,0:T(1,128)S(1)} %bitcast.132), channel_id=1, replica_groups=mesh['section'=4,'expert'=4,'dp'=2] {'dp'}, dimensions={0}, use_global_device_ids=true | all-gather | bytes 1536 | tf_op jit(solution)/shard_map/all_gather | solution.py:154
  39.8 1.4 multiply_convert_fusion.7
  41.7 2.4 %all_gather.23 = bf16[160,2048]{1,0:T(8,128)(2,1)S(1)} all-gather(bf16[80,2048]{1,0:T(8,128)(2,1)S(1)} %convolution_convert_fusion.1), channel_id=1, replica_groups=mesh['section'=4,'expert'=4,'dp'=2] {'dp'}, dimensions={0}, use_global_device_ids=true | all-gather | bytes 983040 | tf_op jit(solution)/shard_map/all_gather | solution.py:149
  44.1 2.4 %all_gather.24 = bf16[160,2048]{1,0:T(8,128)(2,1)S(1)} all-gather(bf16[80,2048]{1,0:T(8,128)(2,1)S(1)} %convolution_convert_fusion), channel_id=1, replica_groups=mesh['section'=4,'expert'=4,'dp'=2] {'dp'}, dimensions={0}, use_global_device_ids=true | all-gather | bytes 983040 | tf_op jit(solution)/shard_map/all_gather | solution.py:148
  46.6 9.3 %fusion.2 = f32[160,3584]{1,0:T(8,128)} fusion(bf16[160,2048]{1,0:T(8,128)(2,1)S(1)} %all_gather.24, bf16[1,2048,3584]{2,1,0:T(8,128)(2,1)} %param.17), kind=kOutput, calls=%fused_computation.2 | convolution fusion | flops 2348810240 | bytes 17629184 | tf_op jit(solution)/shard_map/dot_general | solution.py:65
  55.9 3.9 %fusion.6 = f32[160,3584]{1,0:T(8,128)} fusion(bf16[160,2048]{1,0:T(8,128)(2,1)S(1)} %all_gather.24, bf16[1,2048,3584]{2,1,0:T(8,128)(2,1)S(1)} %bitcast.116), kind=kOutput, calls=%fused_computation.6 | convolution fusion | flops 2348810240 | bytes 17629184 | tf_op jit(solution)/shard_map/dot_general | solution.py:66
  59.8 11.6 %fusion.10 = f32[160,3584]{1,0:T(8,128)} fusion(bf16[160,2048]{1,0:T(8,128)(2,1)S(1)} %all_gather.23, bf16[1,3584,2048]{2,1,0:T(8,128)(2,1)} %param.19), kind=kOutput, calls=%fused_computation.10 | convolution fusion | flops 2348810240 | bytes 17629184 | tf_op jit(solution)/shard_map/dot_general | solution.py:72
  71.4 12.1 %fusion = f32[160,2048]{1,0:T(8,128)S(1)} fusion(bf16[1,2048,3584]{2,1,0:T(8,128)(2,1)} %param.17, f32[160,3584]{1,0:T(8,128)} %fusion.2, f32[160,3584]{1,0:T(8,128)} %fusion.10, f32[160,3584]{1,0:T(8,128)} %fusion.6), kind=kOutput, calls=%fused_computation | convolution fusion | flops 2354544640 | bytes 22872064 | tf_op jit(solution)/shard_map/dot_general | solution.py:75
  83.5 12.8 %fusion.15 = f32[160,2048]{1,0:T(8,128)} fusion(f32[160,2048]{1,0:T(8,128)S(1)} %fusion, bf16[1,2048,3584]{2,1,0:T(8,128)(2,1)} %param.18, f32[160,3584]{1,0:T(8,128)} %fusion.10, f32[160,3584]{1,0:T(8,128)} %fusion.2), kind=kOutput, calls=%fused_computation.13 | convolution fusion | flops 2352578560 | bytes 21889024 | tf_op jit(solution)/shard_map/dot_general | solution.py:75
  96.3 2.2 %reshape.180 = f32[2,80,4,512]{3,2,1,0:T(4,128)S(1)} reshape(f32[160,2048]{1,0:T(8,128)} %fusion.15) | data formatting | bytes 2621440 | tf_op jit(solution)/shard_map/reshape | solution.py:158
  98.5 1.5 multiply_bitcast_fusion
  100.0 1.6 copy.35
  102.1 15.4 %psum.35 = f32[128,64]{0,1:T(8,128)S(1)} all-reduce(f32[128,64]{0,1:T(8,128)S(1)} %fusion.38), channel_id=1, replica_groups=mesh['section'=4,'expert'=4,'dp'=2] {'expert'}, use_global_device_ids=true, to_apply=%region_10.11 | all-reduce | flops 8192 | bytes 65536 | tf_op jit(solution)/shard_map/psum | solution.py:129
  117.5 9.4 %all-gather.1 = bf16[1,2048,64]{1,2,0:T(8,128)(2,1)S(1)} all-gather(bf16[1,512,64]{1,2,0:T(8,128)(2,1)S(1)} %copy-done.5), channel_id=3, replica_groups=mesh['section'=4,'expert'=4,'dp'=2] {'expert'}, dimensions={1}, use_global_device_ids=true | all-gather | bytes 327680 | tf_op jit(solution)/shard_map/all_gather | solution.py:127
  126.9 0.9 convolution_bitcast_fusion
  127.8 1.1 fusion.30
  129.0 9.7 %fusion.20 = f32[160]{0:T(256)S(1)} fusion(bf16[1,3584,2048]{2,1,0:T(8,128)(2,1)} %param.19, bf16[160,2048]{1,0:T(8,128)(2,1)S(1)} %all_gather.23, f32[160,3584]{1,0:T(8,128)} %fusion.6, f32[160,3584]{1,0:T(8,128)} %fusion.2), kind=kOutput, calls=%fused_computation.23 | convolution fusion | flops 2353233664 | bytes 19923584 | tf_op jit(solution)/shard_map/dot_general | solution.py:70
  138.7 2.5 %all-reduce = f32[160]{0:T(256)S(1)} all-reduce(f32[160]{0:T(256)S(1)} %fusion.20), channel_id=5, replica_groups=mesh['section'=4,'expert'=4,'dp'=2] {'dp'}, use_global_device_ids=true, to_apply=%region_12.13.clone | all-reduce | flops 160 | bytes 1280
  142.6 1.4 reduce-scatter.2.cloned.1.call-done
  144.0 1.3 multiply_reduce_fusion.1
  145.3 8.9 %all-reduce.1 = (f32[128,1]{0,1:T(1,128)S(1)}, f32[128,4]{0,1:T(4,128)S(1)}) all-reduce(f32[128,1]{0,1:T(1,128)S(1)} %bitcast.128, f32[128,4]{0,1:T(4,128)S(1)} %broadcast_multiply_fusion), channel_id=1, replica_groups=mesh['section'=4,'expert'=4,'dp'=2] {'expert'}, use_global_device_ids=true, to_apply=%region_17.18 | all-reduce | flops 640 | bytes 5120 | tf_op jit(solution)/shard_map/psum | solution.py:175
  155.1 3.4 %collective-permute-start = (bf16[128,512]{1,0:T(8,128)(2,1)S(1)}, bf16[128,512]{1,0:T(8,128)(2,1)S(1)}, u32[]{:S(2)}, u32[]{:S(2)}) collective-permute-start(bf16[128,512]{1,0:T(8,128)(2,1)S(1)} %fusion.28), channel_id=1, source_target_pairs={{8,0},{16,8},{24,16},{0,24},{9,1},{17,9},{25,17},{1,25},{10,2},{18... | collective-permute-start | bytes 393224 | tf_op jit(solution)/shard_map/ppermute | solution.py:22
  158.5 2.5 %collective-permute-done = bf16[128,512]{1,0:T(8,128)(2,1)S(1)} collective-permute-done((bf16[128,512]{1,0:T(8,128)(2,1)S(1)}, bf16[128,512]{1,0:T(8,128)(2,1)S(1)}, u32[]{:S(2)}, u32[]{:S(2)}) %collective-permute-start) | collective-permute-done | bytes 131104 | tf_op jit(solution)/shard_map/ppermute | solution.py:22
  161.0 0.7 copy.43
  161.7 1.6 copy.44
  163.3 1.6 copy.45
  (87 shorter events, 5.0 us)
Async XLA Ops:
  8.0 93.9 %copy-start = (bf16[1,64,512]{2,1,0:T(8,128)(2,1)S(1)}, bf16[1,64,512]{2,1,0:T(8,128)(2,1)}, u32[]{:S(2)}) copy-start(bf16[1,64,512]{2,1,0:T(8,128)(2,1)} %param.21) | copy-start | bytes 196612
  8.0 12.6 %copy-start.15 = (s32[1,128,2]{1,2,0:T(2,128)S(1)}, s32[1,128,2]{1,2,0:T(2,128)}, u32[]{:S(2)}) copy-start(s32[1,128,2]{1,2,0:T(2,128)} %param.13) | copy-start | bytes 3076
  8.0 13.2 %copy-start.8 = (f32[1,2048]{1,0:T(1,128)S(1)}, f32[1,2048]{1,0:T(1,128)}, u32[]{:S(2)}) copy-start(f32[1,2048]{1,0:T(1,128)} %param.15) | copy-start | bytes 24580
  8.0 135.9 %reduce-scatter.2.cloned.1.call-start = ((), (), s32[]{:S(2)}) async-start(), calls=%async_computation.1 | async-start | bytes 2359296 | tf_op jit(solution)/shard_map/reduce_scatter | solution.py:161
  20.2 3.0 %copy-start.7 = (bf16[1,2048,4]{1,2,0:T(4,128)(2,1)S(1)}, bf16[1,2048,4]{1,2,0:T(4,128)(2,1)}, u32[]{:S(2)}) copy-start(bf16[1,2048,4]{1,2,0:T(4,128)(2,1)} %param.16) | copy-start | bytes 49156
  20.2 5.3 %copy-start.4 = (bf16[1,128,512]{2,1,0:T(8,128)(2,1)S(1)}, bf16[1,128,512]{2,1,0:T(8,128)(2,1)}, u32[]{:S(2)}) copy-start(bf16[1,128,512]{2,1,0:T(8,128)(2,1)} %param.12) | copy-start | bytes 393220
  20.6 4.9 %copy-start.9 = (f32[4]{0:T(128)}, f32[4]{0:T(128)S(1)}, u32[]{:S(2)}) copy-start(f32[4]{0:T(128)S(1)} %compare_convert_fusion) | copy-start | bytes 52
  23.2 32.6 %slice-start = ((s8[14680064]{0:T(1024)(128)(4,1)}), s8[2097152]{0:T(1024)(128)(4,1)S(1)}, s32[]{:S(2)}) async-start(s8[14680064]{0:T(1024)(128)(4,1)} %bitcast.115), calls=%async_computation.3 | async-start | bytes 4194304
  23.6 17.9 %copy-start.11 = (pred[128]{0:T(512)(128)(4,1)}, pred[128]{0:T(512)(128)(4,1)S(1)}, u32[]{:S(2)}) copy-start(pred[128]{0:T(512)(128)(4,1)S(1)} %convert_compare_fusion) | copy-start | bytes 388
  37.1 4.3 %copy-start.3 = (bf16[1,128,2048]{2,1,0:T(8,128)(2,1)S(1)}, bf16[1,128,2048]{2,1,0:T(8,128)(2,1)}, u32[]{:S(2)}) copy-start(bf16[1,128,2048]{2,1,0:T(8,128)(2,1)} %all-gather) | copy-start | bytes 1572868
  39.8 6.8 %copy-start.13 = (s32[128]{0:T(128)}, s32[128]{0:T(128)S(1)}, u32[]{:S(2)}) copy-start(s32[128]{0:T(128)S(1)} %convert_subtract_fusion.1) | copy-start | bytes 1540
  41.7 14.2 %slice-start.1 = ((s8[14680064]{0:T(1024)(128)(4,1)}), s8[4194304]{0:T(1024)(128)(4,1)S(1)}, s32[]{:S(2)}) async-start(s8[14680064]{0:T(1024)(128)(4,1)} %bitcast.115), calls=%async_computation.4 | async-start | bytes 8388608
  46.6 9.3 %slice-start.2 = ((s8[14680064]{0:T(1024)(128)(4,1)}), s8[4194304]{0:T(1024)(128)(4,1)S(1)}, s32[]{:S(2)}) async-start(s8[14680064]{0:T(1024)(128)(4,1)} %bitcast.115), calls=%async_computation.5 | async-start | bytes 8388608
  46.6 9.3 %slice-start.3 = ((s8[14680064]{0:T(1024)(128)(4,1)}), s8[4194304]{0:T(1024)(128)(4,1)S(1)}, s32[]{:S(2)}) async-start(s8[14680064]{0:T(1024)(128)(4,1)} %bitcast.115), calls=%async_computation.6 | async-start | bytes 8388608
  100.0 1.7 copy-start.16
  100.0 17.4 %copy-start.5 = (bf16[1,512,64]{1,2,0:T(8,128)(2,1)S(1)}, bf16[1,512,64]{1,2,0:T(8,128)(2,1)}, u32[]{:S(2)}) copy-start(bf16[1,512,64]{1,2,0:T(8,128)(2,1)} %param.20) | copy-start | bytes 196612
  101.7 59.4 %all-reduce.5.cloned.1.call-start = ((), (), s32[]{:S(2)}) async-start(), calls=%async_computation.2 | async-start | bytes 524288 | tf_op jit(solution)/shard_map/psum | solution.py:140
  129.0 12.2 %copy-start.17 = (u32[32]{0:T(128)S(1)}, u32[32]{0:T(128)}, u32[]{:S(2)}) copy-start(u32[32]{0:T(128)} %constant.93) | copy-start | bytes 388
  129.0 13.3 %copy-start.12 = (pred[128]{0:T(512)(128)(4,1)S(1)}, pred[128]{0:T(512)(128)(4,1)}, u32[]{:S(2)}) copy-start(pred[128]{0:T(512)(128)(4,1)} %copy-done.11) | copy-start | bytes 388
  129.0 13.3 %copy-start.14 = (s32[128]{0:T(128)S(1)}, s32[128]{0:T(128)}, u32[]{:S(2)}) copy-start(s32[128]{0:T(128)} %copy-done.13) | copy-start | bytes 1540
  129.0 13.5 %copy-start.10 = (f32[4]{0:T(128)S(1)}, f32[4]{0:T(128)}, u32[]{:S(2)}) copy-start(f32[4]{0:T(128)} %copy-done.9) | copy-start | bytes 52
  129.0 15.0 %copy-start.1 = (f32[128,2048]{1,0:T(8,128)S(1)}, f32[128,2048]{1,0:T(8,128)}, u32[]{:S(2)}) copy-start(f32[128,2048]{1,0:T(8,128)} %copy.37) | copy-start | bytes 3145732
  129.0 15.0 %copy-start.6 = (bf16[1,512,64]{1,2,0:T(8,128)(2,1)S(1)}, bf16[1,512,64]{1,2,0:T(8,128)(2,1)}, u32[]{:S(2)}) copy-start(bf16[1,512,64]{1,2,0:T(8,128)(2,1)} %param.20) | copy-start | bytes 196612
  129.0 25.2 %copy-start.2 = (f32[4,128,512]{1,2,0:T(8,128)S(1)}, f32[4,128,512]{1,2,0:T(8,128)}, u32[]{:S(2)}) copy-start(f32[4,128,512]{1,2,0:T(8,128)} %get-tuple-element.15) | copy-start | bytes 3145732
  155.1 5.9 %collective-permute-start = (bf16[128,512]{1,0:T(8,128)(2,1)S(1)}, bf16[128,512]{1,0:T(8,128)(2,1)S(1)}, u32[]{:S(2)}, u32[]{:S(2)}) collective-permute-start(bf16[128,512]{1,0:T(8,128)(2,1)S(1)} %fusion.28), channel_id=1, source_target_pairs={{8,0},{16,8},{24,16},{0,24},{9,1},{17,9},{25,17},{1,25},{10,2},{18... | collective-permute-start | bytes 393224 | tf_op jit(solution)/shard_map/ppermute | solution.py:22
Sparse Core Ops, SparseCore 0:
  101.8 42.1 reduce-scatter.1
Sparse Core Ops, SparseCore 1:
  129.0 18.3 all-reduce.4
